TPU v7x, 128 devices: a whole 4x4x4 slice. The times are simulated.
128 devices in a mesh: row: 8 (over y, core), col: 4 (over z), mp: 4 (over x).
Axes of the slice: x: 4, y: 4, z: 4, core: 2. Of those that a mesh axis runs over, the one named last changes fastest.
Arguments:
- hidden: bfloat16 [32768, 3584], P(('row', 'col'), 'mp'), may hold values from -6 to 6
- old_logp: float32 [32768], P(('row', 'col')), may hold values from -0.6 to 0.6
- rewards: float32 [256], P(('row', 'col')), may hold values from -4 to 4
- resp_dest: int32 [256], P(('row', 'col')), may hold values from 0 to 31, as said below
- resp_len: int32 [256], P(('row', 'col')), may hold values from 1 to 128, as said below
- resp_offset: int32 [256], P(('row', 'col')), may hold values from 0 to 511, as said below
- prompt_group: int32 [256], P(('row', 'col')), may hold values from 0 to 31, as said below
- attn_gain: bfloat16 [3584], replicated, may hold values from 0.099609375 to 1.8984375
- w_query: bfloat16 [3584, 3584], P(None, 'mp'), may hold values from -0.09375 to 0.09375
- q_bias: bfloat16 [3584], P('mp'), may hold values from -3 to 3
- w_key: bfloat16 [3584, 512], P(None, 'mp'), may hold values from -0.09375 to 0.09375
- k_bias: bfloat16 [512], P('mp'), may hold values from -6 to 6
- w_value: bfloat16 [3584, 512], P(None, 'mp'), may hold values from -0.09375 to 0.09375
- v_bias: bfloat16 [512], P('mp'), may hold values from -3 to 3
- w_out: bfloat16 [3584, 3584], P('mp'), may hold values from -0.5 to 0.5
- final_gain: bfloat16 [3584], replicated, may hold values from 0.099609375 to 1.8984375
- chosen_rows: bfloat16 [16384, 3584], P(('row', 'col', 'mp')), may hold values from -0.01171875 to 0.01171875
- log_normalizer: float32 [16384], P(('row', 'col', 'mp')), may hold values from -0.6 to 0.6
Outputs:
- objective: float32 [16384], P(('row', 'col', 'mp'))
- loss: float32 [], replicated
Inputs may be any that keep to these rules, and one draw needn't show every extreme that they name: `resp_dest`: ranks are numbered row index * 4 + col index. A rank's responses go to ranks of the same col index: exactly 1 of them to each such rank, itself included; so every rank receives exactly 8 responses. `resp_len`: the responses bound for one rank hold at most 512 tokens together; in every draw some rank's responses fill all 512 positions, and some response has exactly 128. `resp_offset`: responses bound for one rank lie end to end from position 0, without gaps or intersection. `prompt_group`: each of the 32 groups has exactly 8 responses.
All inputs are finite; a program needn't handle non-finite values.
Results may differ from a plain program's by a relative error of at most 0.0019.
Values may be sent and summed in bfloat16 or wider, within the bound.
No kernel may reach another device: no remote copies, remote signals or barrier semaphores. Data moves between devices by JAX's collectives and lax.ppermute only.
A program may use at most 128 MiB of HBM per device.

v0:
```python
import jax
import jax.numpy as jnp
from jax import lax
from jax.sharding import Mesh
from jax.sharding import PartitionSpec as P

HEAD = 128
GROUP_SIZE = 8
ROW = ("row_0", "row_1")
ROW_COL = ("row_0", "row_1", "col")
ROW_COL_MP = ("row_0", "row_1", "col", "mp")
norm_eps = 1e-06
rope_theta = 1000000.0
clip_low = 0.2
clip_high = 0.28
std_floor = 1.0
mask_fill = -1e30


def sent_to_all(value, axis):
    copies = jnp.broadcast_to(value, (lax.axis_size(axis), *value.shape))
    return lax.all_to_all(copies, axis, split_axis=0, concat_axis=0, tiled=True)


def of_everyone(value, axis):
    everything = sent_to_all(value, axis)
    return jnp.sum(everything, axis=0)


def together(arrays, axis):
    ends = [0]
    for a in arrays:
        ends.append(ends[-1] + a.size)
    total = of_everyone(jnp.concatenate([a.ravel() for a in arrays]), axis)
    return tuple((total[b:e].reshape(a.shape) for a, b, e in zip(arrays, ends, ends[1:])))


def over_axes(value, axes):
    for axis in axes:
        value = lax.psum(value, axis)
    return value


def rotary(matrix, positions):
    half_size = matrix.shape[-1] // 2
    exponents = jnp.arange(half_size, dtype=jnp.float32) * (2.0 / matrix.shape[-1])
    frequency = rope_theta ** (-exponents)
    angles = positions[:, None] * frequency[None, :]
    cosine_table = jnp.cos(angles)[:, None, :]
    sine_table = jnp.sin(angles)[:, None, :]
    first_half = matrix[..., :half_size]
    second_half = matrix[..., half_size:]
    return jnp.concatenate(
        [
            first_half * cosine_table - second_half * sine_table,
            second_half * cosine_table + first_half * sine_table,
        ],
        -1,
    )


def body(
    hidden,
    old_logp,
    rewards,
    resp_dest,
    resp_len,
    resp_offset,
    prompt_group,
    attn_gain,
    w_query,
    q_bias,
    w_key,
    k_bias,
    w_value,
    v_bias,
    w_out,
    final_gain,
    chosen_rows,
    log_normalizer,
):
    highest = lax.Precision.HIGHEST
    row_ranks = lax.axis_size(ROW)
    col_ranks = lax.axis_size("col")
    rank_count = row_ranks * col_ranks
    response_count = resp_dest.shape[0]
    per_peer = response_count // row_ranks
    group_count = rank_count * response_count // GROUP_SIZE
    slot_length = hidden.shape[0] // response_count
    feature_count = hidden.shape[1]
    pack_length = response_count * slot_length // 2
    shard_count = lax.axis_size("mp")
    row_count = pack_length // shard_count
    slot_iota = jnp.arange(response_count, dtype=jnp.int32)
    group_iota = jnp.arange(group_count, dtype=jnp.int32)
    dest_row = resp_dest // col_ranks
    earlier = (slot_iota[None, :] < slot_iota[:, None]) & (dest_row[None, :] == dest_row[:, None])
    slot_in_peer = jnp.sum(earlier.astype(jnp.int32), 1)
    send_slot = dest_row * per_peer + slot_in_peer
    selector = send_slot[None, :] == slot_iota[:, None]
    selector_wide = selector.astype(jnp.float32)
    send_rows = jnp.dot(
        selector.astype(jnp.bfloat16),
        hidden.reshape(response_count, slot_length * feature_count),
        preferred_element_type=jnp.float32,
    ).astype(jnp.bfloat16)
    send_rows = send_rows.reshape(row_ranks, per_peer * slot_length, feature_count)
    send_logp = jnp.dot(
        selector_wide, old_logp.reshape(response_count, slot_length), precision=highest
    )
    send_length = jnp.dot(selector_wide, resp_len.astype(jnp.float32), precision=highest)
    send_offset = jnp.dot(selector_wide, resp_offset.astype(jnp.float32), precision=highest)
    member = (prompt_group[:, None] == group_iota[None, :]).astype(jnp.float32)
    send_info = jnp.stack(
        [
            send_length,
            send_offset,
            jnp.dot(selector_wide, rewards, precision=highest),
            jnp.dot(selector_wide, prompt_group.astype(jnp.float32), precision=highest),
        ],
        1,
    )
    send_info = send_info.reshape(row_ranks, per_peer, send_info.shape[1])
    recv_rows = lax.all_to_all(send_rows, ROW, split_axis=0, concat_axis=0, tiled=True)
    recv_logp, recv_info = (
        lax.all_to_all(send_logp, ROW, split_axis=0, concat_axis=0, tiled=True),
        lax.all_to_all(send_info, ROW, split_axis=0, concat_axis=0, tiled=True),
    )
    recv_info = recv_info.reshape(response_count, recv_info.shape[2])
    lengths = recv_info[:, 0].astype(jnp.int32)
    offsets = recv_info[:, 1].astype(jnp.int32)
    slots = jnp.arange(pack_length, dtype=jnp.int32)[:, None]
    covered = (slots >= offsets[None, :]) & (slots < (offsets + lengths)[None, :])
    occupied = jnp.any(covered, 1)
    within_all = slots - offsets[None, :]
    token_index = jnp.sum(jnp.where(covered, slot_iota[None, :] * slot_length + within_all, 0), 1)
    positions = jnp.sum(jnp.where(covered, within_all, 0), 1).astype(jnp.float32)
    segment = jnp.where(occupied, jnp.sum(jnp.where(covered, slot_iota[None, :], 0), 1), -1)
    flat_rows = recv_rows.reshape(-1, feature_count)
    packed = jnp.where(occupied[:, None], flat_rows[token_index], jnp.zeros((), jnp.bfloat16))
    gathered = lax.all_gather(packed, "mp", axis=1, tiled=True)
    inverse = lax.rsqrt(
        jnp.mean(jnp.square(gathered.astype(jnp.float32)), -1, keepdims=True) + norm_eps
    )
    normed = (gathered.astype(jnp.float32) * inverse * attn_gain.astype(jnp.float32)).astype(
        jnp.bfloat16
    )
    heads_local = w_query.shape[1] // HEAD
    key_heads = w_key.shape[1] // HEAD
    queries = jnp.dot(normed, w_query, preferred_element_type=jnp.float32) + q_bias.astype(
        jnp.float32
    )
    queries = rotary(queries.reshape(pack_length, heads_local, HEAD), positions).astype(
        jnp.bfloat16
    )
    key_rows = jnp.dot(normed, w_key, preferred_element_type=jnp.float32) + k_bias.astype(
        jnp.float32
    )
    key_rows = rotary(key_rows.reshape(pack_length, key_heads, HEAD), positions).astype(
        jnp.bfloat16
    )
    value_rows = (
        (jnp.dot(normed, w_value, preferred_element_type=jnp.float32) + v_bias.astype(jnp.float32))
        .astype(jnp.bfloat16)
        .reshape(pack_length, key_heads, HEAD)
    )
    grouped = queries.reshape(pack_length, key_heads, heads_local // key_heads, HEAD)
    block_size = min(512, pack_length)
    scores = jnp.einsum(
        "qkgd,ekd->kgqe", grouped, key_rows, preferred_element_type=jnp.float32
    ) * HEAD ** (-0.5)
    allowed = (segment[0:block_size, None] == segment[None, :block_size]) & (
        jnp.arange(block_size)[None, :] <= jnp.arange(0, block_size)[:, None]
    )
    scores = jnp.where(allowed, scores, mask_fill)
    highest_score = jnp.max(scores, -1, keepdims=True)
    exponent = jnp.exp(scores - highest_score)
    weights = (exponent / jnp.sum(exponent, -1, keepdims=True)).astype(jnp.bfloat16)
    block_out = jnp.einsum(
        "kgqe,ekd->qkgd", weights, value_rows, preferred_element_type=jnp.float32
    )
    pieces = block_out.reshape(block_size, heads_local * HEAD).astype(jnp.bfloat16)
    branch = lax.psum_scatter(
        jnp.dot(pieces, w_out, preferred_element_type=jnp.float32).astype(jnp.bfloat16),
        "mp",
        scatter_dimension=0,
        tiled=True,
    ).astype(jnp.float32)
    own_start = lax.axis_index("mp") * row_count
    residual = lax.dynamic_slice_in_dim(gathered, own_start, row_count, 0)
    residual_out = (residual.astype(jnp.float32) + branch).astype(jnp.bfloat16)
    final_rows = residual_out.astype(jnp.float32)
    final_inverse = lax.rsqrt(jnp.mean(final_rows * final_rows, -1, keepdims=True) + norm_eps)
    logits = jnp.sum(
        final_rows
        * final_inverse
        * final_gain.astype(jnp.float32)
        * chosen_rows.astype(jnp.float32),
        -1,
    )
    own_covered = lax.dynamic_slice_in_dim(covered, own_start, row_count, 0)
    own_occupied = lax.dynamic_slice_in_dim(occupied, own_start, row_count, 0)
    own_token = lax.dynamic_slice_in_dim(token_index, own_start, row_count, 0)
    own_old = jnp.where(own_occupied, recv_logp.reshape(-1)[own_token], 0.0)
    totals, squares = together(
        (
            jnp.dot(rewards, member, precision=highest),
            jnp.dot(rewards * rewards, member, precision=highest),
        ),
        ROW_COL,
    )
    means = totals / GROUP_SIZE
    variance = jnp.maximum(squares / GROUP_SIZE - means * means, 0.0)
    means, scales = (means, jnp.maximum(jnp.sqrt(variance), std_floor))
    pair_member = (recv_info[:, 3].astype(jnp.int32)[:, None] == group_iota[None, :]).astype(
        jnp.float32
    )
    pair_adv = (recv_info[:, 2] - jnp.dot(pair_member, means, precision=highest)) / jnp.dot(
        pair_member, scales, precision=highest
    )
    token_adv = jnp.sum(jnp.where(own_covered, pair_adv[None, :], 0.0), 1)
    ratios = jnp.exp(logits - log_normalizer - own_old)
    bounded = jnp.clip(ratios, 1.0 - clip_low, 1.0 + clip_high)
    objective = jnp.where(own_occupied, jnp.minimum(ratios * token_adv, bounded * token_adv), 0.0)
    loss_sum, counted = (
        over_axes(jnp.sum(objective), ROW_COL_MP),
        over_axes(jnp.sum(own_occupied.astype(jnp.float32)), ROW_COL_MP),
    )
    return (objective, -loss_sum / counted)


def solution(mesh):
    finer = Mesh(
        mesh.devices.reshape(4, 2, mesh.shape["col"], mesh.shape["mp"]),
        ("row_0", "row_1", "col", "mp"),
    )
    placed = (
        P(ROW_COL, "mp"),
        P(ROW_COL),
        P(ROW_COL),
        P(ROW_COL),
        P(ROW_COL),
        P(ROW_COL),
        P(ROW_COL),
        P(),
        P(None, "mp"),
        P("mp"),
        P(None, "mp"),
        P("mp"),
        P(None, "mp"),
        P("mp"),
        P("mp", None),
        P(),
        P(ROW_COL_MP, None),
        P(ROW_COL_MP),
    )
    return jax.shard_map(
        body, mesh=finer, in_specs=placed, out_specs=(P(ROW_COL_MP), P()), check_vma=False
    )
```

profile of v0, /device:TPU:0, one launch (start us, length us, event | category | flops | bytes accessed | tf_op | source)
XLA Modules:
  0.0 239.6 jit_solution(6732604042234698789)
XLA Ops:
  12.6 4.6 %all-to-all-start = ((f32[8,1,4]{2,1,0:T(1,128)}), f32[8,1,4]{2,1,0:T(1,128)S(1)}, u32[]{:S(2)}, u32[]{:S(2)}) async-start(f32[8,1,4]{2,1,0:T(1,128)} %copy.51), calls=%async_computation | async-start | bytes 8192 | tf_op jit(solution)/shard_map/all_to_all | solution.py:127
  17.2 2.3 reshape.258
  22.5 4.0 %all-to-all-start.1 = ((bf16[8,128,896]{2,1,0:T(8,128)(2,1)}), bf16[8,128,896]{2,1,0:T(8,128)(2,1)S(1)}, u32[]{:S(2)}, u32[]{:S(2)}) async-start(bf16[8,128,896]{2,1,0:T(8,128)(2,1)} %copy.53), calls=%async_computation.1 | async-start | bytes 3670016 | tf_op jit(solution)/shard_map/all_to_all | solution.py:124
  28.0 22.9 %all-to-all-done.1 = bf16[8,128,896]{2,1,0:T(8,128)(2,1)S(1)} async-done(((bf16[8,128,896]{2,1,0:T(8,128)(2,1)}), bf16[8,128,896]{2,1,0:T(8,128)(2,1)S(1)}, u32[]{:S(2)}, u32[]{:S(2)}) %all-to-all-start.1) | async-done | bytes 1835040 | tf_op jit(solution)/shard_map/all_to_all | solution.py:124
  50.9 2.8 %gather_fusion = bf16[512,896]{1,0:T(8,128)(2,1)} fusion(bf16[1024,896]{1,0:T(8,128)(2,1)S(1)} %bitcast.121, s32[1024]{0:T(1024)S(1)} %pad_clamp_fusion.1), kind=kCustom, calls=%fused_computation | custom fusion | bytes 1837056 | tf_op jit(solution)/shard_map/gather | solution.py:140
  53.6 2.3 broadcast_select_fusion
  58.4 41.8 %all-gather.2.cloned.1.call-done = bf16[512,3584]{1,0:T(8,128)(2,1)} async-done(((bf16[512,896]{1,0:T(8,128)(2,1)}), bf16[512,3584]{1,0:T(8,128)(2,1)}) %all-gather.2.cloned.1.call-update) | async-done | bytes 3670032 | tf_op jit(solution)/shard_map/all_gather | solution.py:141
  100.3 3.0 %fusion = f32[512]{0:T(512)S(1)} fusion(bf16[512,3584]{1,0:T(8,128)(2,1)} %all-gather.2.cloned.1.call-done), kind=kLoop, calls=%fused_computation.5 | loop fusion | flops 5504512 | bytes 3672064 | tf_op jit(solution)/shard_map/reduce_sum | solution.py:143
  103.9 8.1 %convolution_add_fusion = f32[512,896]{1,0:T(8,128)} fusion(bf16[3584,896]{1,0:T(8,128)(2,1)} %param.26, f32[896]{0:T(1024)S(1)} %convert_element_type.138, bf16[512,3584]{1,0:T(8,128)(2,1)S(1)} %copy-done.2, f32[3584]{0:T(1024)S(1)} %convert_element_type.132, f32[512]{0:T(512)S(1)} %add_rsqrt_fusion), kind=kOutput, calls=%fused_computation.26 | convolution fusion | flops 3296133120 | bytes 11947520 | tf_op jit(solution)/shard_map/dot_general | solution.py:150
  116.9 3.0 %copy.68 = f32[512,7,64]{2,0,1:T(8,128)} copy(f32[512,7,64]{0,2,1:T(8,128)} %get-tuple-element.17) | data formatting | bytes 1835008
  119.9 3.9 %fusion.15 = f32[512,1,128]{0,2,1:T(8,128)S(1)} fusion(bf16[3584,128]{1,0:T(8,128)(2,1)} %param.28, f32[128]{0:T(128)} %convert_element_type.136, bf16[512,3584]{1,0:T(8,128)(2,1)} %all-gather.2.cloned.1.call-done, f32[3584]{0:T(1024)} %copy-done.5, f32[512]{0:T(512)} %copy-done.13), kind=kOutput, calls=%fused_computation.29 | convolution fusion | flops 477167616 | bytes 4866560 | tf_op jit(solution)/shard_map/dot_general | solution.py:156
  127.0 3.0 %copy-done.1 = f32[512,512,7]{1,0,2:T(8,128)} copy-done((f32[512,512,7]{1,0,2:T(8,128)}, f32[512,512,7]{1,0,2:T(8,128)S(1)}, u32[]{:S(2)}) %copy-start.1) | copy-done | bytes 7340056
  131.6 7.6 %fusion.12 = bf16[128,7,512]{2,0,1:T(8,128)(2,1)S(1)} fusion(f32[7,512]{1,0:T(8,128)S(1)} %fusion.3, f32[7,512]{1,0:T(8,128)S(1)} %get-tuple-element.28, f32[512,512,7]{1,0,2:T(8,128)} %copy-done.1, pred[512,512]{0,1:T(8,128)(4,1)S(1)} %fusion.20, bf16[3584,128]{1,0:T(8,128)(2,1)S(1)} %copy-done, f32[128]{0:T(128)S(1)} %copy-done.23, ...), kind=kOutput, calls=%fused_computation.27 | convolution fusion | flops 956628992 | bytes 13152768 | tf_op jit(solution)/shard_map/kgqe,ekd->qkgd/dot_general | solution.py:179
  139.2 8.3 %convolution_convert_fusion.1 = bf16[512,3584]{1,0:T(8,128)(2,1)} fusion(bf16[512,896]{0,1:T(8,128)(2,1)S(1)} %bitcast.130, bf16[896,3584]{1,0:T(8,128)(2,1)} %param.32), kind=kOutput, calls=%fused_computation.12 | convolution fusion | flops 3290169344 | bytes 11010048 | tf_op jit(solution)/shard_map/dot_general | solution.py:184
  148.9 4.3 %all-to-all-start.2 = ((f32[8,1,128]{2,1,0:T(1,128)}), f32[8,1,128]{2,1,0:T(1,128)S(1)}, u32[]{:S(2)}, u32[]{:S(2)}) async-start(f32[8,1,128]{2,1,0:T(1,128)} %bitcast.34), calls=%async_computation.3 | async-start | bytes 8192 | tf_op jit(solution)/shard_map/all_to_all | solution.py:126
  153.7 4.7 %all-to-all-done.2 = f32[8,1,128]{2,1,0:T(1,128)S(1)} async-done(((f32[8,1,128]{2,1,0:T(1,128)}), f32[8,1,128]{2,1,0:T(1,128)S(1)}, u32[]{:S(2)}, u32[]{:S(2)}) %all-to-all-start.2) | async-done | bytes 4128 | tf_op jit(solution)/shard_map/all_to_all | solution.py:126
  159.0 5.4 %all-to-all-start.3 = ((f32[32,1,64]{2,1,0:T(1,128)}), f32[32,1,64]{2,1,0:T(1,128)S(1)}, u32[]{:S(2)}, u32[]{:S(2)}) async-start(f32[32,1,64]{2,1,0:T(1,128)} %broadcast_in_dim.65), calls=%async_computation.4 | async-start | bytes 32768 | tf_op jit(solution)/shard_map/all_to_all | solution.py:22
  165.5 6.4 %all-to-all-done.3 = f32[32,1,64]{2,1,0:T(1,128)S(1)} async-done(((f32[32,1,64]{2,1,0:T(1,128)}), f32[32,1,64]{2,1,0:T(1,128)S(1)}, u32[]{:S(2)}, u32[]{:S(2)}) %all-to-all-start.3) | async-done | bytes 8224 | tf_op jit(solution)/shard_map/all_to_all | solution.py:22
  173.0 17.5 %reduce-scatter.2.cloned.1.call-done = bf16[128,3584]{1,0:T(8,128)(2,1)} async-done(((bf16[512,3584]{1,0:T(8,128)(2,1)}), bf16[128,3584]{1,0:T(8,128)(2,1)}) %reduce-scatter.2.cloned.1.call-update) | async-done | bytes 917520 | tf_op jit(solution)/shard_map/reduce_scatter | solution.py:183
  192.3 2.1 fusion.11
  195.6 11.2 %all-reduce.2 = (f32[]{:T(128)}, f32[]{:T(128)}) all-reduce(f32[]{:T(128)} %get-tuple-element.13, f32[]{:T(128)} %get-tuple-element.27), channel_id=1, replica_groups=mesh['row_0'=4,'row_1'=2,'col'=4,'mp'=4] {'row_0'}, use_global_device_ids=true, to_apply=%region_14.15 | all-reduce | flops 2 | bytes 16 | tf_op jit(solution)/shard_map/psum | solution.py:40
  206.8 3.1 %all-reduce.3 = (f32[]{:T(128)}, f32[]{:T(128)}) all-reduce(f32[]{:T(128)} %get-tuple-element.9, f32[]{:T(128)} %get-tuple-element.10), channel_id=1, replica_groups=mesh['row_0'=4,'row_1'=2,'col'=4,'mp'=4] {'row_1'}, use_global_device_ids=true, to_apply=%region_15.16 | all-reduce | flops 2 | bytes 16 | tf_op jit(solution)/shard_map/psum | solution.py:40
  209.9 11.3 %all-reduce.1 = (f32[]{:T(128)}, f32[]{:T(128)}) all-reduce(f32[]{:T(128)} %get-tuple-element.11, f32[]{:T(128)} %get-tuple-element.12), channel_id=1, replica_groups=mesh['row_0'=4,'row_1'=2,'col'=4,'mp'=4] {'col'}, use_global_device_ids=true, to_apply=%region_16.17 | all-reduce | flops 2 | bytes 16 | tf_op jit(solution)/shard_map/psum | solution.py:40
  221.2 9.2 %all-reduce = (f32[]{:T(128)}, f32[]{:T(128)}) all-reduce(f32[]{:T(128)} %get-tuple-element.7, f32[]{:T(128)} %get-tuple-element.8), channel_id=1, replica_groups=mesh['row_0'=4,'row_1'=2,'col'=4,'mp'=4] {'mp'}, use_global_device_ids=true, to_apply=%region_17.18 | all-reduce | flops 2 | bytes 16 | tf_op jit(solution)/shard_map/psum | solution.py:40
  (103 shorter events, 30.2 us)
Async XLA Ops:
  7.2 124.4 %copy-start = (bf16[3584,128]{1,0:T(8,128)(2,1)S(1)}, bf16[3584,128]{1,0:T(8,128)(2,1)}, u32[]{:S(2)}) copy-start(bf16[3584,128]{1,0:T(8,128)(2,1)} %param.30) | copy-start | bytes 2752516
  8.8 11.4 %copy-start.15 = (s32[8]{0:T(128)}, s32[8]{0:T(128)S(1)}, u32[]{:S(2)}) copy-start(s32[8]{0:T(128)S(1)} %fusion.84) | copy-start | bytes 100
  12.6 9.9 %all-to-all-start = ((f32[8,1,4]{2,1,0:T(1,128)}), f32[8,1,4]{2,1,0:T(1,128)S(1)}, u32[]{:S(2)}, u32[]{:S(2)}) async-start(f32[8,1,4]{2,1,0:T(1,128)} %copy.51), calls=%async_computation | async-start | bytes 8192 | tf_op jit(solution)/shard_map/all_to_all | solution.py:127
  22.5 28.4 %all-to-all-start.1 = ((bf16[8,128,896]{2,1,0:T(8,128)(2,1)}), bf16[8,128,896]{2,1,0:T(8,128)(2,1)S(1)}, u32[]{:S(2)}, u32[]{:S(2)}) async-start(bf16[8,128,896]{2,1,0:T(8,128)(2,1)} %copy.53), calls=%async_computation.1 | async-start | bytes 3670016 | tf_op jit(solution)/shard_map/all_to_all | solution.py:124
  26.5 73.8 %all-gather.2.cloned.1.call-start = ((), (), s32[]{:S(2)}) async-start(), calls=%async_computation.5 | async-start | bytes 4587520 | tf_op jit(solution)/shard_map/all_gather | solution.py:141
  50.9 5.1 %copy-start.7 = (bf16[3584]{0:T(1024)(128)(2,1)S(1)}, bf16[3584]{0:T(1024)(128)(2,1)}, u32[]{:S(2)}) copy-start(bf16[3584]{0:T(1024)(128)(2,1)} %param.25) | copy-start | bytes 21508
  50.9 5.1 %copy-start.12 = (bf16[896]{0:T(1024)(128)(2,1)S(1)}, bf16[896]{0:T(1024)(128)(2,1)}, u32[]{:S(2)}) copy-start(bf16[896]{0:T(1024)(128)(2,1)} %param.27) | copy-start | bytes 5380
  50.9 5.2 %copy-start.19 = (bf16[128]{0:T(256)(128)(2,1)S(1)}, bf16[128]{0:T(256)(128)(2,1)}, u32[]{:S(2)}) copy-start(bf16[128]{0:T(256)(128)(2,1)} %param.29) | copy-start | bytes 772
  50.9 5.8 %copy-start.20 = (bf16[128]{0:T(256)(128)(2,1)S(1)}, bf16[128]{0:T(256)(128)(2,1)}, u32[]{:S(2)}) copy-start(bf16[128]{0:T(256)(128)(2,1)} %param.31) | copy-start | bytes 772
  55.9 134.5 %reduce-scatter.2.cloned.1.call-start = ((), (), s32[]{:S(2)}) async-start(), calls=%async_computation.6 | async-start | bytes 4587520 | tf_op jit(solution)/shard_map/reduce_scatter | solution.py:183
  56.0 47.2 %copy-start.5 = (f32[3584]{0:T(1024)}, f32[3584]{0:T(1024)S(1)}, u32[]{:S(2)}) copy-start(f32[3584]{0:T(1024)S(1)} %convert_element_type.132) | copy-start | bytes 43012
  100.3 3.6 %copy-start.2 = (bf16[512,3584]{1,0:T(8,128)(2,1)S(1)}, bf16[512,3584]{1,0:T(8,128)(2,1)}, u32[]{:S(2)}) copy-start(bf16[512,3584]{1,0:T(8,128)(2,1)} %all-gather.2.cloned.1.call-done) | copy-start | bytes 11010052
  119.9 3.9 %copy-start.11 = (f32[64]{0:T(128)S(1)}, f32[64]{0:T(128)}, u32[]{:S(2)}) copy-start(f32[64]{0:T(128)} %copy-done.10) | copy-start | bytes 772
  119.9 4.5 %copy-start.3 = (f32[512,7,64]{2,0,1:T(8,128)S(1)}, f32[512,7,64]{2,0,1:T(8,128)}, u32[]{:S(2)}) copy-start(f32[512,7,64]{2,0,1:T(8,128)} %copy.68) | copy-start | bytes 2752516
  127.0 3.0 %copy-start.1 = (f32[512,512,7]{1,0,2:T(8,128)}, f32[512,512,7]{1,0,2:T(8,128)S(1)}, u32[]{:S(2)}) copy-start(f32[512,512,7]{1,0,2:T(8,128)S(1)} %get-tuple-element.29) | copy-start | bytes 22020100
  130.0 1.6 copy-start.23
  147.5 5.7 %copy-start.8 = (bf16[3584]{0:T(1024)(128)(2,1)S(1)}, bf16[3584]{0:T(1024)(128)(2,1)}, u32[]{:S(2)}) copy-start(bf16[3584]{0:T(1024)(128)(2,1)} %param.33) | copy-start | bytes 21508
  147.5 5.7 %copy-start.21 = (s32[8]{0:T(128)S(1)}, s32[8]{0:T(128)}, u32[]{:S(2)}) copy-start(s32[8]{0:T(128)} %param.24) | copy-start | bytes 100
  147.5 5.7 %copy-start.22 = (f32[8]{0:T(128)S(1)}, f32[8]{0:T(128)}, u32[]{:S(2)}) copy-start(f32[8]{0:T(128)} %param.20) | copy-start | bytes 100
  147.5 24.4 %copy-start.18 = (s32[8]{0:T(128)S(1)}, s32[8]{0:T(128)}, u32[]{:S(2)}) copy-start(s32[8]{0:T(128)} %get-tuple-element.23) | copy-start | bytes 100
  147.5 44.8 %copy-start.4 = (bf16[128,3584]{1,0:T(8,128)(2,1)S(1)}, bf16[128,3584]{1,0:T(8,128)(2,1)}, u32[]{:S(2)}) copy-start(bf16[128,3584]{1,0:T(8,128)(2,1)} %param.34) | copy-start | bytes 2752516
  148.1 46.3 %copy-start.17 = (f32[128]{0:T(128)S(1)}, f32[128]{0:T(128)}, u32[]{:S(2)}) copy-start(f32[128]{0:T(128)} %param.35) | copy-start | bytes 1540
  148.9 9.6 %all-to-all-start.2 = ((f32[8,1,128]{2,1,0:T(1,128)}), f32[8,1,128]{2,1,0:T(1,128)S(1)}, u32[]{:S(2)}, u32[]{:S(2)}) async-start(f32[8,1,128]{2,1,0:T(1,128)} %bitcast.34), calls=%async_computation.3 | async-start | bytes 8192 | tf_op jit(solution)/shard_map/all_to_all | solution.py:126
  159.0 12.8 %all-to-all-start.3 = ((f32[32,1,64]{2,1,0:T(1,128)}), f32[32,1,64]{2,1,0:T(1,128)S(1)}, u32[]{:S(2)}, u32[]{:S(2)}) async-start(f32[32,1,64]{2,1,0:T(1,128)} %broadcast_in_dim.65), calls=%async_computation.4 | async-start | bytes 32768 | tf_op jit(solution)/shard_map/all_to_all | solution.py:22
  (6 other events, 6.4 us)
Sparse Core Ops, SparseCore 0:
  56.1 44.1 all-gather.1
  147.7 42.7 reduce-scatter.1
where the time goes:
time: 240 us
  waiting for transfers between devices  94.2 us (39%)
  matrix products  35.1 us (15%)
  blocking collectives  34.8 us (14%)
  local copies, waits for them, and re-layouts  21.2 us (9%)
  other arithmetic  19.2 us (8%)
  starting transfers between devices  18.4 us (8%)
  between operations  16.8 us (7%)
    all_gather x1, waiting for transfers between devices, body(): gathered = lax.all_gather(packed, 'mp', axis=1, tiled=True)  41.8 us
    psum x4, blocking collectives, over_axes(): value = lax.psum(value, axis)  34.8 us
    all_to_all x1, waiting for transfers between devices, body(): lax.all_to_all(send_rows, ROW, split_axis=0, concat_axis=0, tiled=True)  22.9 us
    reduce_scatter x1, waiting for transfers between devices, body(): lax.psum_scatter(jnp.dot(pieces, w_out, preferred_element_type=jnp.float3...  17.5 us
    unnamed x50, local copies, waits for them, and re-layouts  8.94 us
    dot_general x1, matrix products, body(): jnp.dot(pieces, w_out, preferred_element_type=jnp.float32)  8.28 us
    dot_general x1, matrix products, body(): jnp.dot(normed, w_query, preferred_element_type=jnp.float32)  8.08 us
    dot_general x1, matrix products, body(): jnp.einsum('kgqe,ekd->qkgd', weights, value_rows, preferred_element_type=...  7.58 us
  transfers between devices with their start and end apart: 6, of which 6 were waited for; matrix products, arithmetic and copies ran while one was open for 5% of the time, Pallas kernels for 0%

commit v1 on v0

--- a/solution.py
+++ b/solution.py
@@ -37,7 +37,7 @@
 
 def over_axes(value, axes):
     for axis in axes:
-        value = lax.psum(value, axis)
+        value = jnp.sum(lax.all_gather(value, axis), axis=0)
     return value
 
 

time: 240 us -> 256 us (1.067)
  local copies, waits for them, and re-layouts: 21.2 us -> 35.1 us
  other arithmetic: 19.2 us -> 24.1 us
  blocking collectives: 34.8 us -> 32.1 us
    psum x4 -> x0, blocking collectives: 34.8 us -> none  [over_axes(): value = lax.psum(value, axis)]
    unnamed x0 -> x4, blocking collectives: none -> 32.1 us
    unnamed x50 -> x78, local copies, waits for them, and re-layouts: 8.94 us -> 22.9 us
    reduce_sum x0 -> x8, other arithmetic: none -> 4.79 us  [over_axes(): value = jnp.sum(lax.all_gather(value, axis), axis=0)]
where the time goes in v1:
time: 256 us; the launch traced here: 255 us
  waiting for transfers between devices  93.3 us (36%)
  local copies, waits for them, and re-layouts  35.1 us (14%)
  matrix products  35.1 us (14%)
  blocking collectives  32.1 us (13%)
  other arithmetic  24.1 us (9%)
  starting transfers between devices  18.6 us (7%)
  between operations  16.9 us (7%)
    all_gather x1, waiting for transfers between devices, body(): gathered = lax.all_gather(packed, 'mp', axis=1, tiled=True)  41.8 us
    unnamed x4, blocking collectives  32.1 us
    all_to_all x1, waiting for transfers between devices, body(): lax.all_to_all(send_rows, ROW, split_axis=0, concat_axis=0, tiled=True)  22.9 us
    unnamed x78, local copies, waits for them, and re-layouts  22.9 us
    reduce_scatter x1, waiting for transfers between devices, body(): lax.psum_scatter(jnp.dot(pieces, w_out, preferred_element_type=jnp.float3...  17.3 us
    dot_general x1, matrix products, body(): jnp.dot(pieces, w_out, preferred_element_type=jnp.float32)  8.28 us
    dot_general x1, matrix products, body(): jnp.dot(normed, w_query, preferred_element_type=jnp.float32)  8.08 us
    dot_general x1, matrix products, body(): jnp.einsum('kgqe,ekd->qkgd', weights, value_rows, preferred_element_type=...  7.58 us
  transfers between devices with their start and end apart: 6, of which 6 were waited for; matrix products, arithmetic and copies ran while one was open for 5% of the time, Pallas kernels for 0%

profile of v1, /device:TPU:0, one launch (start us, length us, event | category | flops | bytes accessed | tf_op | source)
XLA Modules:
  0.0 255.2 jit_solution(8067595644753070933)
XLA Ops:
  12.6 4.6 %all-to-all-start = ((f32[8,1,4]{2,1,0:T(1,128)}), f32[8,1,4]{2,1,0:T(1,128)S(1)}, u32[]{:S(2)}, u32[]{:S(2)}) async-start(f32[8,1,4]{2,1,0:T(1,128)} %copy.51), calls=%async_computation | async-start | bytes 8192 | tf_op jit(solution)/shard_map/all_to_all | solution.py:127
  17.2 2.3 reshape.258
  22.5 4.0 %all-to-all-start.1 = ((bf16[8,128,896]{2,1,0:T(8,128)(2,1)}), bf16[8,128,896]{2,1,0:T(8,128)(2,1)S(1)}, u32[]{:S(2)}, u32[]{:S(2)}) async-start(bf16[8,128,896]{2,1,0:T(8,128)(2,1)} %copy.53), calls=%async_computation.1 | async-start | bytes 3670016 | tf_op jit(solution)/shard_map/all_to_all | solution.py:124
  28.0 22.9 %all-to-all-done.1 = bf16[8,128,896]{2,1,0:T(8,128)(2,1)S(1)} async-done(((bf16[8,128,896]{2,1,0:T(8,128)(2,1)}), bf16[8,128,896]{2,1,0:T(8,128)(2,1)S(1)}, u32[]{:S(2)}, u32[]{:S(2)}) %all-to-all-start.1) | async-done | bytes 1835040 | tf_op jit(solution)/shard_map/all_to_all | solution.py:124
  50.9 2.8 %gather_fusion = bf16[512,896]{1,0:T(8,128)(2,1)} fusion(bf16[1024,896]{1,0:T(8,128)(2,1)S(1)} %bitcast.133, s32[1024]{0:T(1024)S(1)} %pad_clamp_fusion.1), kind=kCustom, calls=%fused_computation | custom fusion | bytes 1837056 | tf_op jit(solution)/shard_map/gather | solution.py:140
  53.6 2.3 broadcast_select_fusion
  58.4 41.8 %all-gather.2.cloned.1.call-done = bf16[512,3584]{1,0:T(8,128)(2,1)} async-done(((bf16[512,896]{1,0:T(8,128)(2,1)}), bf16[512,3584]{1,0:T(8,128)(2,1)}) %all-gather.2.cloned.1.call-update) | async-done | bytes 3670032 | tf_op jit(solution)/shard_map/all_gather | solution.py:141
  100.3 3.0 %fusion = f32[512]{0:T(512)S(1)} fusion(bf16[512,3584]{1,0:T(8,128)(2,1)} %all-gather.2.cloned.1.call-done), kind=kLoop, calls=%fused_computation.5 | loop fusion | flops 5504512 | bytes 3672064 | tf_op jit(solution)/shard_map/reduce_sum | solution.py:143
  103.9 8.1 %convolution_add_fusion = f32[512,896]{1,0:T(8,128)} fusion(bf16[3584,896]{1,0:T(8,128)(2,1)} %param.26, f32[896]{0:T(1024)S(1)} %convert_element_type.138, bf16[512,3584]{1,0:T(8,128)(2,1)S(1)} %copy-done.2, f32[3584]{0:T(1024)S(1)} %convert_element_type.132, f32[512]{0:T(512)S(1)} %add_rsqrt_fusion), kind=kOutput, calls=%fused_computation.26 | convolution fusion | flops 3296133120 | bytes 11947520 | tf_op jit(solution)/shard_map/dot_general | solution.py:150
  116.9 3.0 %copy.68 = f32[512,7,64]{2,0,1:T(8,128)} copy(f32[512,7,64]{0,2,1:T(8,128)} %get-tuple-element.17) | data formatting | bytes 1835008
  119.9 3.9 %fusion.15 = f32[512,1,128]{0,2,1:T(8,128)S(1)} fusion(bf16[3584,128]{1,0:T(8,128)(2,1)} %param.28, f32[128]{0:T(128)} %convert_element_type.136, bf16[512,3584]{1,0:T(8,128)(2,1)} %all-gather.2.cloned.1.call-done, f32[3584]{0:T(1024)} %copy-done.5, f32[512]{0:T(512)} %copy-done.13), kind=kOutput, calls=%fused_computation.29 | convolution fusion | flops 477167616 | bytes 4866560 | tf_op jit(solution)/shard_map/dot_general | solution.py:156
  127.0 3.0 %copy-done.1 = f32[512,512,7]{1,0,2:T(8,128)} copy-done((f32[512,512,7]{1,0,2:T(8,128)}, f32[512,512,7]{1,0,2:T(8,128)S(1)}, u32[]{:S(2)}) %copy-start.1) | copy-done | bytes 7340056
  131.6 7.6 %fusion.12 = bf16[128,7,512]{2,0,1:T(8,128)(2,1)S(1)} fusion(f32[7,512]{1,0:T(8,128)S(1)} %fusion.3, f32[7,512]{1,0:T(8,128)S(1)} %get-tuple-element.28, f32[512,512,7]{1,0,2:T(8,128)} %copy-done.1, pred[512,512]{0,1:T(8,128)(4,1)S(1)} %fusion.20, bf16[3584,128]{1,0:T(8,128)(2,1)S(1)} %copy-done, f32[128]{0:T(128)S(1)} %copy-done.27, ...), kind=kOutput, calls=%fused_computation.27 | convolution fusion | flops 956628992 | bytes 13152768 | tf_op jit(solution)/shard_map/kgqe,ekd->qkgd/dot_general | solution.py:179
  139.2 8.3 %convolution_convert_fusion.1 = bf16[512,3584]{1,0:T(8,128)(2,1)} fusion(bf16[512,896]{0,1:T(8,128)(2,1)S(1)} %bitcast.142, bf16[896,3584]{1,0:T(8,128)(2,1)} %param.32), kind=kOutput, calls=%fused_computation.12 | convolution fusion | flops 3290169344 | bytes 11010048 | tf_op jit(solution)/shard_map/dot_general | solution.py:184
  148.9 4.3 %all-to-all-start.2 = ((f32[8,1,128]{2,1,0:T(1,128)}), f32[8,1,128]{2,1,0:T(1,128)S(1)}, u32[]{:S(2)}, u32[]{:S(2)}) async-start(f32[8,1,128]{2,1,0:T(1,128)} %bitcast.34), calls=%async_computation.3 | async-start | bytes 8192 | tf_op jit(solution)/shard_map/all_to_all | solution.py:126
  154.4 4.1 %all-to-all-done.2 = f32[8,1,128]{2,1,0:T(1,128)S(1)} async-done(((f32[8,1,128]{2,1,0:T(1,128)}), f32[8,1,128]{2,1,0:T(1,128)S(1)}, u32[]{:S(2)}, u32[]{:S(2)}) %all-to-all-start.2) | async-done | bytes 4128 | tf_op jit(solution)/shard_map/all_to_all | solution.py:126
  159.1 5.6 %all-to-all-start.3 = ((f32[32,1,64]{2,1,0:T(1,128)}), f32[32,1,64]{2,1,0:T(1,128)S(1)}, u32[]{:S(2)}, u32[]{:S(2)}) async-start(f32[32,1,64]{2,1,0:T(1,128)} %broadcast_in_dim.65), calls=%async_computation.4 | async-start | bytes 32768 | tf_op jit(solution)/shard_map/all_to_all | solution.py:22
  165.7 6.4 %all-to-all-done.3 = f32[32,1,64]{2,1,0:T(1,128)S(1)} async-done(((f32[32,1,64]{2,1,0:T(1,128)}), f32[32,1,64]{2,1,0:T(1,128)S(1)}, u32[]{:S(2)}, u32[]{:S(2)}) %all-to-all-start.3) | async-done | bytes 8224 | tf_op jit(solution)/shard_map/all_to_all | solution.py:22
  173.2 17.3 %reduce-scatter.2.cloned.1.call-done = bf16[128,3584]{1,0:T(8,128)(2,1)} async-done(((bf16[512,3584]{1,0:T(8,128)(2,1)}), bf16[128,3584]{1,0:T(8,128)(2,1)}) %reduce-scatter.2.cloned.1.call-update) | async-done | bytes 917520 | tf_op jit(solution)/shard_map/reduce_scatter | solution.py:183
  192.4 2.1 fusion.11
  199.3 10.4 %all-reduce.10 = (f32[4]{0:T(128)S(1)}, f32[4]{0:T(128)S(1)}) all-reduce(f32[4]{0:T(128)S(1)} %dynamic-update-slice, f32[4]{0:T(128)S(1)} %dynamic-update-slice.4), channel_id=1, replica_groups=mesh['row_0'=4,'row_1'=2,'col'=4,'mp'=4] {'row_0'}, use_global_device_ids=true, to_apply=%add | all-reduce | flops 8 | bytes 64
  214.4 2.4 all-reduce.11
  221.5 10.6 %all-reduce.9 = (f32[4]{0:T(128)S(1)}, f32[4]{0:T(128)S(1)}) all-reduce(f32[4]{0:T(128)S(1)} %dynamic-update-slice.2, f32[4]{0:T(128)S(1)} %dynamic-update-slice.6), channel_id=1, replica_groups=mesh['row_0'=4,'row_1'=2,'col'=4,'mp'=4] {'col'}, use_global_device_ids=true, to_apply=%add.2 | all-reduce | flops 8 | bytes 64
  236.1 8.6 %all-reduce.8 = (f32[4]{0:T(128)S(1)}, f32[4]{0:T(128)S(1)}) all-reduce(f32[4]{0:T(128)S(1)} %dynamic-update-slice.3, f32[4]{0:T(128)S(1)} %dynamic-update-slice.7), channel_id=1, replica_groups=mesh['row_0'=4,'row_1'=2,'col'=4,'mp'=4] {'mp'}, use_global_device_ids=true, to_apply=%add.3 | all-reduce | flops 8 | bytes 64
  (139 shorter events, 49.0 us)
Async XLA Ops:
  7.2 124.4 %copy-start = (bf16[3584,128]{1,0:T(8,128)(2,1)S(1)}, bf16[3584,128]{1,0:T(8,128)(2,1)}, u32[]{:S(2)}) copy-start(bf16[3584,128]{1,0:T(8,128)(2,1)} %param.30) | copy-start | bytes 2752516
  8.8 11.4 %copy-start.15 = (s32[8]{0:T(128)}, s32[8]{0:T(128)S(1)}, u32[]{:S(2)}) copy-start(s32[8]{0:T(128)S(1)} %fusion.84) | copy-start | bytes 100
  12.6 9.9 %all-to-all-start = ((f32[8,1,4]{2,1,0:T(1,128)}), f32[8,1,4]{2,1,0:T(1,128)S(1)}, u32[]{:S(2)}, u32[]{:S(2)}) async-start(f32[8,1,4]{2,1,0:T(1,128)} %copy.51), calls=%async_computation | async-start | bytes 8192 | tf_op jit(solution)/shard_map/all_to_all | solution.py:127
  22.5 28.4 %all-to-all-start.1 = ((bf16[8,128,896]{2,1,0:T(8,128)(2,1)}), bf16[8,128,896]{2,1,0:T(8,128)(2,1)S(1)}, u32[]{:S(2)}, u32[]{:S(2)}) async-start(bf16[8,128,896]{2,1,0:T(8,128)(2,1)} %copy.53), calls=%async_computation.1 | async-start | bytes 3670016 | tf_op jit(solution)/shard_map/all_to_all | solution.py:124
  26.5 73.8 %all-gather.2.cloned.1.call-start = ((), (), s32[]{:S(2)}) async-start(), calls=%async_computation.5 | async-start | bytes 4587520 | tf_op jit(solution)/shard_map/all_gather | solution.py:141
  50.9 5.1 %copy-start.7 = (bf16[3584]{0:T(1024)(128)(2,1)S(1)}, bf16[3584]{0:T(1024)(128)(2,1)}, u32[]{:S(2)}) copy-start(bf16[3584]{0:T(1024)(128)(2,1)} %param.25) | copy-start | bytes 21508
  50.9 5.1 %copy-start.12 = (bf16[896]{0:T(1024)(128)(2,1)S(1)}, bf16[896]{0:T(1024)(128)(2,1)}, u32[]{:S(2)}) copy-start(bf16[896]{0:T(1024)(128)(2,1)} %param.27) | copy-start | bytes 5380
  50.9 5.2 %copy-start.19 = (bf16[128]{0:T(256)(128)(2,1)S(1)}, bf16[128]{0:T(256)(128)(2,1)}, u32[]{:S(2)}) copy-start(bf16[128]{0:T(256)(128)(2,1)} %param.29) | copy-start | bytes 772
  50.9 5.8 %copy-start.20 = (bf16[128]{0:T(256)(128)(2,1)S(1)}, bf16[128]{0:T(256)(128)(2,1)}, u32[]{:S(2)}) copy-start(bf16[128]{0:T(256)(128)(2,1)} %param.31) | copy-start | bytes 772
  55.9 134.6 %reduce-scatter.2.cloned.1.call-start = ((), (), s32[]{:S(2)}) async-start(), calls=%async_computation.6 | async-start | bytes 4587520 | tf_op jit(solution)/shard_map/reduce_scatter | solution.py:183
  56.0 47.2 %copy-start.5 = (f32[3584]{0:T(1024)}, f32[3584]{0:T(1024)S(1)}, u32[]{:S(2)}) copy-start(f32[3584]{0:T(1024)S(1)} %convert_element_type.132) | copy-start | bytes 43012
  119.9 4.5 %copy-start.3 = (f32[512,7,64]{2,0,1:T(8,128)S(1)}, f32[512,7,64]{2,0,1:T(8,128)}, u32[]{:S(2)}) copy-start(f32[512,7,64]{2,0,1:T(8,128)} %copy.68) | copy-start | bytes 2752516
  147.5 5.7 %copy-start.8 = (bf16[3584]{0:T(1024)(128)(2,1)S(1)}, bf16[3584]{0:T(1024)(128)(2,1)}, u32[]{:S(2)}) copy-start(bf16[3584]{0:T(1024)(128)(2,1)} %param.33) | copy-start | bytes 21508
  147.5 5.7 %copy-start.26 = (u32[128]{0:T(128)S(1)}, u32[128]{0:T(128)}, u32[]{:S(2)}) copy-start(u32[128]{0:T(128)} %constant.74) | copy-start | bytes 1540
  147.5 6.4 %copy-start.21 = (s32[8]{0:T(128)S(1)}, s32[8]{0:T(128)}, u32[]{:S(2)}) copy-start(s32[8]{0:T(128)} %param.24) | copy-start | bytes 100
  147.5 6.4 %copy-start.22 = (f32[8]{0:T(128)S(1)}, f32[8]{0:T(128)}, u32[]{:S(2)}) copy-start(f32[8]{0:T(128)} %param.20) | copy-start | bytes 100
  147.5 24.6 %copy-start.18 = (s32[8]{0:T(128)S(1)}, s32[8]{0:T(128)}, u32[]{:S(2)}) copy-start(s32[8]{0:T(128)} %get-tuple-element.23) | copy-start | bytes 100
  147.5 44.8 %copy-start.4 = (bf16[128,3584]{1,0:T(8,128)(2,1)S(1)}, bf16[128,3584]{1,0:T(8,128)(2,1)}, u32[]{:S(2)}) copy-start(bf16[128,3584]{1,0:T(8,128)(2,1)} %param.34) | copy-start | bytes 2752516
  148.1 46.3 %copy-start.17 = (f32[128]{0:T(128)S(1)}, f32[128]{0:T(128)}, u32[]{:S(2)}) copy-start(f32[128]{0:T(128)} %param.35) | copy-start | bytes 1540
  148.1 50.5 %copy-start.25 = (u32[128]{0:T(128)S(1)}, u32[128]{0:T(128)}, u32[]{:S(2)}) copy-start(u32[128]{0:T(128)} %constant.79) | copy-start | bytes 1540
  148.1 65.6 %copy-start.24 = (u32[128]{0:T(128)S(1)}, u32[128]{0:T(128)}, u32[]{:S(2)}) copy-start(u32[128]{0:T(128)} %constant.84) | copy-start | bytes 1540
  148.2 72.7 %copy-start.23 = (u32[128]{0:T(128)S(1)}, u32[128]{0:T(128)}, u32[]{:S(2)}) copy-start(u32[128]{0:T(128)} %constant.89) | copy-start | bytes 1540
  148.9 9.6 %all-to-all-start.2 = ((f32[8,1,128]{2,1,0:T(1,128)}), f32[8,1,128]{2,1,0:T(1,128)S(1)}, u32[]{:S(2)}, u32[]{:S(2)}) async-start(f32[8,1,128]{2,1,0:T(1,128)} %bitcast.34), calls=%async_computation.3 | async-start | bytes 8192 | tf_op jit(solution)/shard_map/all_to_all | solution.py:126
  159.1 13.0 %all-to-all-start.3 = ((f32[32,1,64]{2,1,0:T(1,128)}), f32[32,1,64]{2,1,0:T(1,128)S(1)}, u32[]{:S(2)}, u32[]{:S(2)}) async-start(f32[32,1,64]{2,1,0:T(1,128)} %broadcast_in_dim.65), calls=%async_computation.4 | async-start | bytes 32768 | tf_op jit(solution)/shard_map/all_to_all | solution.py:22
  (10 other events, 18.4 us)
Sparse Core Ops, SparseCore 0:
  56.1 44.1 all-gather.1
  147.7 42.7 reduce-scatter.1
